TPU v7x, 32 devices: a whole 2x2x4 slice. The times are simulated.
32 devices in a mesh: seq: 8 (over z, y), grp: 4 (over x, core).
Axes of the slice: x: 2, y: 2, z: 4, core: 2. Of those that a mesh axis runs over, the one named last changes fastest.
Arguments:
- hidden: bfloat16 [256, 8192], P('grp', 'seq'), may hold values from -6 to 6
- w_qkv: bfloat16 [8192, 10240], P('seq', 'grp'), may hold values from -0.0625 to 0.0625
- b_qkv: float32 [10240], P('grp'), may hold values from -3 to 3
- w_out: bfloat16 [8192, 8192], P('seq', 'grp'), may hold values from -0.0625 to 0.0625
- k_cache: bfloat16 [4, 32768, 1024], P('grp', 'seq'), may hold values from -600 to 600
- v_cache: bfloat16 [4, 32768, 1024], P('grp', 'seq'), may hold values from -6 to 6
- lengths: int32 [256], replicated, may hold values from 1 to 16384, as said below
- page_table: int32 [256, 128], replicated, may hold values from -1 to 255, as said below
- positions: int32 [3, 256], replicated, may hold values from 0 to 4095
- group_of: int32 [256], replicated, may hold values from 0 to 3, as said below
Outputs:
- mixed: bfloat16 [256, 8192], P('seq', 'grp')
Inputs may be any that keep to these rules, and one draw needn't show every extreme that they name: `group_of`: each group serves exactly 64 requests. `lengths`: each group has a request of exactly 16384 cached positions. `page_table`: entry j of row r is the page of request r's group pool (page p lies on that group's device p // 32 of seq) that holds its positions j * 128 to (j + 1) * 128 - 1, for j < ceil(lengths[r] / 128); later entries are -1; no page belongs to two requests.
All inputs are finite; a program needn't handle non-finite values.
Results may differ from a plain program's by a relative error of at most 0.015.
The roundings to bfloat16 on the way count: a program that leaves them out, or rounds other values in their place, can miss the bound.
Values may be sent and summed in bfloat16 or wider, within the bound.
A program may use at most 128 MiB of HBM per device.

v0:
```python
import math
import jax
import jax.numpy as jnp
from jax import lax
from jax.sharding import PartitionSpec as P

HQ = 64
KVH = 8
HD = 128
PAGE = 128
rope_base = 1000000.0
neg_fill = -1e30


def rotate_heads(values, places, col_start, head_dim, turned):
    row_count, col_count = values.shape
    columns = col_start + jnp.arange(col_count, dtype=jnp.int32)
    within = columns % head_dim
    freq_index = within % (head_dim // 2)
    inverse_freq = jnp.exp(freq_index.astype(jnp.float32) * (-2.0 * math.log(rope_base) / head_dim))
    section = jnp.where(
        freq_index < head_dim // 8,
        0,
        jnp.where(freq_index < head_dim // 8 + 3 * head_dim // 16, 1, 2),
    )
    place_float = places.astype(jnp.float32)
    chosen = jnp.where(
        section[None, :] == 0,
        place_float[0][:, None],
        jnp.where(section[None, :] == 1, place_float[1][:, None], place_float[2][:, None]),
    )
    angles = chosen * inverse_freq[None, :]
    halves = values.reshape(row_count, col_count // head_dim, 2, head_dim // 2)
    partner = jnp.concatenate([-halves[:, :, 1:], halves[:, :, :1]], axis=2).reshape(
        row_count, col_count
    )
    rotated = values * jnp.cos(angles) + partner * jnp.sin(angles)
    return jnp.where((columns < turned)[None, :], rotated, values)


def shards(hidden, w_qkv, b_qkv, w_out, k_cache, v_cache, lengths, page_table, positions, group_of):
    seq_count = lax.axis_size("seq")
    grp_count = lax.axis_size("grp")
    seq_index = lax.axis_index("seq")
    grp_index = lax.axis_index("grp")
    request_total = group_of.shape[0]
    group_size = request_total // grp_count
    col_count = w_qkv.shape[1]
    col_start = grp_index * col_count
    turned = (HQ + KVH) * HD
    group_q = HQ // KVH
    score_scale = HD ** (-0.5)
    partial_sum = jnp.dot(
        lax.all_gather(hidden, "grp", axis=0, tiled=True), w_qkv, preferred_element_type=jnp.float32
    )
    request_ids = jnp.arange(request_total, dtype=jnp.int32)
    before = (group_of[None, :] < group_of[:, None]) | (group_of[None, :] == group_of[:, None]) & (
        request_ids[None, :] < request_ids[:, None]
    )
    restore = jnp.sum(before.astype(jnp.int32), axis=1)
    placed_at = restore[None, :] == request_ids[:, None]
    served_order = jnp.sum(jnp.where(placed_at, request_ids[None, :], 0), axis=1)
    served_ids = lax.dynamic_slice_in_dim(served_order, grp_index * group_size, group_size, 0)
    summed = lax.psum(partial_sum, "seq")
    fresh_rows = rotate_heads(summed + b_qkv[None, :], positions, col_start, HD, turned).astype(
        jnp.bfloat16
    )
    outgoing = fresh_rows[served_order].reshape(grp_count, group_size, col_count)
    incoming = lax.all_to_all(outgoing, "grp", split_axis=0, concat_axis=2, tiled=True)
    served_rows = incoming.reshape(group_size, grp_count * col_count)
    query_rows = served_rows[:, : HQ * HD]
    key_new = served_rows[:, HQ * HD : turned]
    value_new = served_rows[:, turned:]
    served_len = lengths[served_ids]
    served_table = page_table[served_ids]
    most_pages = page_table.shape[1]
    page_counts = (served_len + PAGE - 1) // PAGE
    logical = jnp.arange(most_pages, dtype=jnp.int32)
    pool_pages = k_cache.shape[1] // PAGE
    local_page = served_table - seq_index * pool_pages
    usable = (
        (logical[None, :] < page_counts[:, None]) & (local_page >= 0) & (local_page < pool_pages)
    )
    pool_ids = jnp.arange(pool_pages, dtype=jnp.int32)
    matched = usable[:, :, None] & (local_page[:, :, None] == pool_ids[None, None, :])
    owner_ids = jnp.arange(group_size, dtype=jnp.int32)
    page_owner = jnp.max(jnp.where(matched, owner_ids[:, None, None], -1), axis=(0, 1))
    page_number = jnp.max(jnp.where(matched, logical[None, :, None], 0), axis=(0, 1))
    present = page_owner >= 0
    holder = jnp.maximum(page_owner, 0)
    page_query = query_rows[holder].reshape(pool_pages, KVH, group_q, HD)
    page_keys = k_cache[0].reshape(pool_pages, PAGE, KVH, HD)
    page_values = v_cache[0].reshape(pool_pages, PAGE, KVH, HD)
    scores = (
        jnp.einsum("pkgd,ptkd->pkgt", page_query, page_keys, preferred_element_type=jnp.float32)
        * score_scale
    )
    places_in = page_number[:, None] * PAGE + jnp.arange(PAGE, dtype=jnp.int32)[None, :]
    alive_rows = present[:, None] & (places_in < served_len[holder][:, None])
    alive_wide = alive_rows[:, None, None, :]
    page_max = jnp.max(jnp.where(alive_wide, scores, neg_fill), axis=3)
    weights = jnp.exp(jnp.where(alive_wide, scores - page_max[..., None], neg_fill))
    page_total = jnp.sum(weights, axis=3).reshape(pool_pages, HQ)
    page_out = jnp.einsum(
        "pkgt,ptkd->pkgd",
        weights.astype(jnp.bfloat16),
        page_values,
        preferred_element_type=jnp.float32,
    ).reshape(pool_pages, HQ, HD)
    page_max = page_max.reshape(pool_pages, HQ)
    member = page_owner[:, None] == owner_ids[None, :]
    local_max = jnp.max(jnp.where(member[:, :, None], page_max[:, None, :], neg_fill), axis=0)
    factor = jnp.where(present[:, None], jnp.exp(page_max - local_max[holder]), 0.0)
    member_float = member.astype(jnp.float32)
    local_total = jnp.einsum(
        "pr,ph->rh", member_float, page_total * factor, precision=lax.Precision.HIGHEST
    )
    local_out = jnp.einsum(
        "pr,pe->re",
        member_float,
        (page_out * factor[..., None]).reshape(pool_pages, HQ * HD),
        precision=lax.Precision.HIGHEST,
    )
    new_score = (
        jnp.einsum(
            "rkgd,rkd->rkg",
            query_rows.reshape(group_size, KVH, group_q, HD),
            key_new.reshape(group_size, KVH, HD),
            preferred_element_type=jnp.float32,
        ).reshape(group_size, HQ)
        * score_scale
    )
    head_share = HQ // seq_count
    head_start = seq_index * head_share
    value_heads = jnp.broadcast_to(
        value_new.reshape(group_size, KVH, 1, HD), (group_size, KVH, group_q, HD)
    ).reshape(group_size, HQ, HD)
    value_here = lax.dynamic_slice_in_dim(value_heads, head_start, head_share, 1).astype(
        jnp.float32
    )
    new_here = lax.dynamic_slice_in_dim(new_score, head_start, head_share, 1)
    peak_score = lax.pmax(jnp.maximum(local_max, new_score), "seq")
    kept_scale = jnp.exp(local_max - peak_score)
    scaled_out = (local_out.reshape(group_size, HQ, HD) * kept_scale[..., None]).reshape(
        group_size, HQ * HD
    )
    shared_out, shared_total = (
        lax.psum_scatter(scaled_out, "seq", scatter_dimension=1, tiled=True),
        lax.psum_scatter(local_total * kept_scale, "seq", scatter_dimension=1, tiled=True),
    )
    peak_here = lax.dynamic_slice_in_dim(peak_score, head_start, head_share, 1)
    fresh_weight = jnp.exp(new_here - peak_here)
    denominator = shared_total + fresh_weight
    numerator = (
        shared_out.reshape(group_size, head_share, HD) + fresh_weight[..., None] * value_here
    )
    attended = (
        (numerator / denominator[..., None])
        .reshape(group_size, head_share * HD)
        .astype(jnp.bfloat16)
    )
    gathered = lax.all_gather(attended, "grp", axis=0, tiled=True)
    by_request = gathered[restore]
    return lax.psum_scatter(
        jnp.dot(by_request, w_out, preferred_element_type=jnp.float32).astype(jnp.bfloat16),
        "seq",
        scatter_dimension=0,
        tiled=True,
    )


def solution(mesh):
    placed = (
        P("grp", "seq"),
        P("seq", "grp"),
        P("grp"),
        P("seq", "grp"),
        P("grp", "seq", None),
        P("grp", "seq", None),
        P(),
        P(),
        P(),
        P(),
    )
    return jax.shard_map(
        shards, mesh=mesh, in_specs=placed, out_specs=P("seq", "grp"), check_vma=False
    )
```

profile of v0, /device:TPU:0, one launch (start us, length us, event | category | flops | bytes accessed | tf_op | source)
XLA Modules:
  0.0 401.6 jit_solution(12910051012480212838)
XLA Ops:
  6.5 9.0 %all_gather.6 = bf16[256,1024]{1,0:T(8,128)(2,1)S(1)} all-gather(bf16[64,1024]{1,0:T(8,128)(2,1)} %param.10), channel_id=1, replica_groups=mesh['seq'=8,'grp'=4] {'grp'}, dimensions={0}, use_global_device_ids=true | all-gather | bytes 655360 | tf_op jit(solution)/shard_map/all_gather | solution.py:54
  15.5 5.5 %fusion.40 = f32[256,2560]{1,0:T(8,128)} fusion(bf16[256,1024]{1,0:T(8,128)(2,1)S(1)} %all_gather.6, bf16[1024,2560]{1,0:T(8,128)(2,1)} %param.11), kind=kOutput, calls=%fused_computation.102 | convolution fusion | flops 1342177280 | bytes 8388608 | tf_op jit(solution)/shard_map/dot_general | solution.py:53
  21.1 0.6 copy-done.12
  22.1 0.8 gather_fusion
  22.9 0.6 gather_fusion.1
  23.5 0.6 compare_select_fusion
  24.3 0.6 select_reduce_fusion.2
  24.9 113.1 %all-reduce.3.cloned.1.call-done = f32[256,2560]{1,0:T(8,128)} async-done(((f32[256,2560]{1,0:T(8,128)}), f32[256,2560]{1,0:T(8,128)}) %all-reduce.3.cloned.1.call-update) | async-done | bytes 2621456 | tf_op jit(solution)/shard_map/psum | solution.py:64
  138.0 3.6 broadcast_add_fusion
  141.6 2.1 copy.46
  144.1 2.1 copy.47
  146.2 11.8 %select_convert_fusion = bf16[256,2560]{1,0:T(8,128)(2,1)S(1)} fusion(f32[256,2560]{1,0:T(8,128)} %copy.47, f32[2560]{0:T(1024)S(1)} %multiply_exponential_fusion, f32[256]{0:T(256)S(1)} %bitcast.123, f32[256]{0:T(256)S(1)} %bitcast.124, f32[256]{0:T(256)S(1)} %bitcast.122, pred[2560]{0:T(1024)(128)(4,1)S(1)} %get-tuple-element.26, ...), kind=kLoop, calls=%fused_computation.12 | loop fusion | flops 5898240 | bytes 6584832 | tf_op jit(solution)/shard_map/convert_element_type | solution.py:65
  158.0 2.5 gather_fusion.3
  160.5 3.5 all-to-all-start
  164.4 0.7 gather_fusion.2
  165.1 8.8 %copy.68 = bf16[512,8,8,128]{3,2,1,0:T(8,128)(2,1)} copy(bf16[512,8,8,128]{3,1,2,0:T(8,128)(2,1)} %bitcast.100) | data formatting | bytes 16777216
  173.8 8.8 %copy.69 = bf16[512,8,8,128]{3,2,1,0:T(8,128)(2,1)} copy(bf16[512,8,8,128]{3,1,2,0:T(8,128)(2,1)} %bitcast.101) | data formatting | bytes 16777216
  182.6 0.7 iota_compare_fusion.4
  183.4 1.0 copy.48
  184.6 0.3 slice_bitcast_fusion.1
  184.9 1.7 gather_fusion.4
  186.6 1.2 copy.67
  187.8 6.9 %select_reduce_fusion.1 = (f32[32,8,8]{2,1,0:T(8,128)S(1)}, f32[32,8,8,128]{3,2,1,0:T(8,128)S(1)}) fusion(pred[32,128]{1,0:T(8,128)(4,1)S(1)} %fusion.25, bf16[32,8,8,128]{3,2,1,0:T(8,128)(2,1)S(1)} %bitcast.109, bf16[32,128,8,128]{3,2,1,0:T(8,128)(2,1)} %bitcast.97), kind=kOutput, calls=%fused_computation.26 | convolution fusion | flops 67893248 | bytes 9973760 | tf_op jit(solution)/shard_map/pkgd,ptkd->pkgt/dot_general | solution.py:95
  194.7 0.7 copy.51
  195.4 0.8 copy.53
  196.3 1.6 select_reduce_fusion
  197.9 2.0 gather_fusion.5
  199.9 1.4 copy.56
  201.4 0.7 slice_bitcast_fusion
  202.1 1.4 exponential_select_fusion
  203.5 0.3 copy.72
  203.8 1.0 reshape.359
  204.8 0.7 fusion.41
  205.6 35.0 %pmax.7 = f32[64,64]{0,1:T(8,128)S(1)} all-reduce(f32[64,64]{0,1:T(8,128)S(1)} %fusion.38), channel_id=1, replica_groups=mesh['seq'=8,'grp'=4] {'seq'}, use_global_device_ids=true, to_apply=%region_7.8 | all-reduce | flops 4096 | bytes 32768 | tf_op jit(solution)/shard_map/pmax | solution.py:142
  240.7 6.1 %fusion = f32[32,8,8,128]{3,2,1,0:T(8,128)S(1)} fusion(bf16[32,128,8,128]{3,2,1,0:T(8,128)(2,1)} %bitcast.96, f32[32,8,8,128]{3,2,1,0:T(8,128)S(1)} %get-tuple-element.21, f32[32,8,8]{2,1,0:T(8,128)S(1)} %get-tuple-element.20, pred[32,128]{1,0:T(8,128)(4,1)S(1)} %copy-done.6), kind=kOutput, calls=%fused_computation.7 | convolution fusion | flops 67895296 | bytes 10498048 | tf_op jit(solution)/shard_map/pkgt,ptkd->pkgd/dot_general | solution.py:104
  246.7 0.3 mul.108
  247.1 2.5 multiply_bitcast_fusion
  249.6 1.5 copy.96
  251.2 0.7 dynamic-slice
  252.5 0.7 fusion.11
  253.6 33.8 %all-reduce = f32[64,64]{0,1:T(8,128)S(1)} all-reduce(f32[64,64]{0,1:T(8,128)S(1)} %convolution_multiply_fusion), channel_id=3, replica_groups=mesh['seq'=8,'grp'=4] {'seq'}, use_global_device_ids=true, to_apply=%region_10.11.clone | all-reduce | flops 4096 | bytes 32768
  287.7 0.3 broadcast_bitcast_fusion
  288.0 29.7 %reduce-scatter.3.cloned.1.call-done = f32[64,1024]{1,0:T(8,128)} async-done(((f32[64,8192]{1,0:T(8,128)}), f32[64,1024]{1,0:T(8,128)}) %reduce-scatter.3.cloned.1.call-update) | async-done | bytes 262160 | tf_op jit(solution)/shard_map/reduce_scatter | solution.py:148
  317.7 1.0 copy.73
  318.9 7.2 %all_gather.7 = bf16[256,1024]{1,0:T(8,128)(2,1)S(1)} all-gather(bf16[64,1024]{1,0:T(8,128)(2,1)S(1)} %bitcast.113), channel_id=1, replica_groups=mesh['seq'=8,'grp'=4] {'grp'}, dimensions={0}, use_global_device_ids=true | all-gather | bytes 655360 | tf_op jit(solution)/shard_map/all_gather | solution.py:162
  326.1 1.2 gather_fusion.6
  327.3 4.4 %convolution_convert_fusion = bf16[256,2048]{1,0:T(8,128)(2,1)} fusion(bf16[256,1024]{1,0:T(8,128)(2,1)S(1)} %gather_fusion.6, bf16[1024,2048]{1,0:T(8,128)(2,1)} %param.13), kind=kOutput, calls=%fused_computation.13 | convolution fusion | flops 1074266112 | bytes 5767168 | tf_op jit(solution)/shard_map/dot_general | solution.py:165
  331.7 63.4 %reduce-scatter.5.cloned.1.call-done = bf16[32,2048]{1,0:T(8,128)(2,1)} async-done(((bf16[256,2048]{1,0:T(8,128)(2,1)}), bf16[32,2048]{1,0:T(8,128)(2,1)}) %reduce-scatter.5.cloned.1.call-update) | async-done | bytes 131088 | tf_op jit(solution)/shard_map/reduce_scatter | solution.py:164
  (73 shorter events, 2.7 us)
Async XLA Ops:
  6.5 16.4 %copy-start = (s32[256,128]{1,0:T(8,128)S(1)}, s32[256,128]{1,0:T(8,128)}, u32[]{:S(2)}) copy-start(s32[256,128]{1,0:T(8,128)} %param.17) | copy-start | bytes 393220
  6.5 131.5 %all-reduce.3.cloned.1.call-start = ((), (), s32[]{:S(2)}) async-start(), calls=%async_computation.3 | async-start | bytes 5242880 | tf_op jit(solution)/shard_map/psum | solution.py:64
  21.0 0.7 copy-start.12
  21.0 1.1 copy-start.2
  21.0 2.5 copy-start.13
  21.0 117.0 %copy-start.8 = (f32[2560]{0:T(1024)S(1)}, f32[2560]{0:T(1024)}, u32[]{:S(2)}) copy-start(f32[2560]{0:T(1024)} %param.12) | copy-start | bytes 30724
  24.9 157.7 %copy-start.9 = (s32[32]{0:T(128)}, s32[32]{0:T(128)S(1)}, u32[]{:S(2)}) copy-start(s32[32]{0:T(128)S(1)} %get-tuple-element.6) | copy-start | bytes 388
  160.5 22.8 %all-to-all-start = ((bf16[4,64,2560]{2,1,0:T(8,128)(2,1)}), bf16[4,64,2560]{2,1,0:T(8,128)(2,1)S(1)}, u32[]{:S(2)}, u32[]{:S(2)}) async-start(bf16[4,64,2560]{2,1,0:T(8,128)(2,1)} %bitcast.8), calls=%async_computation | async-start | bytes 2621440 | tf_op jit(solution)/shard_map/all_to_all | solution.py:69
  164.1 153.6 %reduce-scatter.3.cloned.1.call-start = ((), (), s32[]{:S(2)}) async-start(), calls=%async_computation.4 | async-start | bytes 2359296 | tf_op jit(solution)/shard_map/reduce_scatter | solution.py:148
  164.3 20.6 %copy-start.11 = (s32[1024]{0:T(1024)}, s32[1024]{0:T(1024)S(1)}, u32[]{:S(2)}) copy-start(s32[1024]{0:T(1024)S(1)} %pad_clamp_fusion.2) | copy-start | bytes 12292
  182.6 2.0 copy-start.15
  183.4 4.4 %copy-start.5 = (pred[32,128]{1,0:T(8,128)(4,1)}, pred[32,128]{1,0:T(8,128)(4,1)S(1)}, u32[]{:S(2)}) copy-start(pred[32,128]{1,0:T(8,128)(4,1)S(1)} %fusion.25) | copy-start | bytes 12292
  202.1 3.5 copy-start.4
  203.5 37.2 %copy-start.6 = (pred[32,128]{1,0:T(8,128)(4,1)S(1)}, pred[32,128]{1,0:T(8,128)(4,1)}, u32[]{:S(2)}) copy-start(pred[32,128]{1,0:T(8,128)(4,1)} %copy-done.5) | copy-start | bytes 12292
  240.7 6.1 %copy-start.7 = (f32[32,64]{1,0:T(8,128)S(1)}, f32[32,64]{1,0:T(8,128)}, u32[]{:S(2)}) copy-start(f32[32,64]{1,0:T(8,128)} %exponential_select_fusion) | copy-start | bytes 24580
  240.7 6.4 %copy-start.10 = (s32[32]{0:T(128)S(1)}, s32[32]{0:T(128)}, u32[]{:S(2)}) copy-start(s32[32]{0:T(128)} %copy-done.9) | copy-start | bytes 388
  249.6 1.6 copy-start.16
  249.6 2.9 copy-start.14
  251.1 36.6 %copy-start.3 = (bf16[8,8,8,128]{3,1,2,0:T(8,128)(2,1)S(1)}, bf16[8,8,8,128]{3,1,2,0:T(8,128)(2,1)}, u32[]{:S(2)}) copy-start(bf16[8,8,8,128]{3,1,2,0:T(8,128)(2,1)} %get-tuple-element.13) | copy-start | bytes 393220
  251.1 143.9 %reduce-scatter.5.cloned.1.call-start = ((), (), s32[]{:S(2)}) async-start(), calls=%async_computation.5 | async-start | bytes 1179648 | tf_op jit(solution)/shard_map/reduce_scatter | solution.py:164
  326.1 69.0 %copy-start.1 = (s32[256,128]{1,0:T(8,128)S(1)}, s32[256,128]{1,0:T(8,128)}, u32[]{:S(2)}) copy-start(s32[256,128]{1,0:T(8,128)} %param.17) | copy-start | bytes 393220
Sparse Core Ops, SparseCore 0:
  21.2 116.7 all-reduce.2
  251.2 66.3 reduce-scatter.2
  331.8 63.1 reduce-scatter.4
where the time goes:
time: 403 us; the launch traced here: 402 us
  waiting for transfers between devices  206 us (51%)
  blocking collectives  85 us (21%)
  local copies, waits for them, and re-layouts  43.9 us (11%)
  matrix products  26.3 us (7%)
  other arithmetic  22.2 us (6%)
  between operations  14.2 us (4%)
    psum x1, waiting for transfers between devices, shards(): summed = lax.psum(partial_sum, 'seq')  113 us
    reduce_scatter x1, waiting for transfers between devices, shards(): lax.psum_scatter(jnp.dot(by_request, w_out, preferred_element_type=jnp.fl...  63.4 us
    pmax x1, blocking collectives, shards(): peak_score = lax.pmax(jnp.maximum(local_max, new_score), 'seq')  35 us
    unnamed x1, blocking collectives  33.8 us
    reduce_scatter x1, waiting for transfers between devices, shards(): lax.psum_scatter(scaled_out, 'seq', scatter_dimension=1, tiled=True)  29.7 us
    unnamed x45, local copies, waits for them, and re-layouts  22.6 us
    convert_element_type x1, other arithmetic, shards(): rotate_heads(summed + b_qkv[None, :], positions, col_start, HD, turned)  11.8 us
    all_gather x1, blocking collectives, shards(): lax.all_gather(hidden, 'grp', axis=0, tiled=True)  8.97 us
  transfers between devices with their start and end apart: 4, of which 3 were waited for; matrix products, arithmetic and copies ran while one was open for 6% of the time, Pallas kernels for 0%

commit v1 on v0

--- a/solution.py
+++ b/solution.py
@@ -10,6 +10,14 @@
 PAGE = 128
 rope_base = 1000000.0
 neg_fill = -1e30
+
+
+def added_up(value, axis):
+    peers, acc = (lax.axis_size(axis), value)
+    for far in [1 << k for k in range(peers.bit_length() - 1)]:
+        swap = [(i, i ^ far) for i in range(peers)]
+        acc = acc + lax.ppermute(acc, axis, swap)
+    return acc
 
 
 def rotate_heads(values, places, col_start, head_dim, turned):
@@ -61,7 +69,7 @@
     placed_at = restore[None, :] == request_ids[:, None]
     served_order = jnp.sum(jnp.where(placed_at, request_ids[None, :], 0), axis=1)
     served_ids = lax.dynamic_slice_in_dim(served_order, grp_index * group_size, group_size, 0)
-    summed = lax.psum(partial_sum, "seq")
+    summed = added_up(partial_sum, "seq")
     fresh_rows = rotate_heads(summed + b_qkv[None, :], positions, col_start, HD, turned).astype(
         jnp.bfloat16
     )

time: 403 us -> 521 us (1.29)
  waiting for transfers between devices: 206 us -> 316 us
  starting transfers between devices: 3.81 us -> 9.68 us
    ppermute x0 -> x3, waiting for transfers between devices: none -> 223 us  [added_up(): acc = acc + lax.ppermute(acc, axis, swap)]
    psum x1 -> x0, waiting for transfers between devices: 113 us -> none  [shards(): summed = lax.psum(partial_sum, 'seq')]
    ppermute x0 -> x3, starting transfers between devices: none -> 5.88 us  [added_up(): acc = acc + lax.ppermute(acc, axis, swap)]
    unnamed x45 -> x49, local copies, waits for them, and re-layouts: 22.6 us -> 22 us
  transfers between devices with their start and end apart: 4 -> 6, of which waited for: 3 -> 5; matrix products, arithmetic and copies ran while one was open for 6% -> 5% of each run, Pallas kernels for 0% -> 0%
where the time goes in v1:
time: 521 us; the launch traced here: 520 us
  waiting for transfers between devices  316 us (61%)
  blocking collectives  87.3 us (17%)
  local copies, waits for them, and re-layouts  43.5 us (8%)
  matrix products  24.8 us (5%)
  other arithmetic  23.9 us (5%)
  between operations  14.6 us (3%)
  starting transfers between devices  9.68 us (2%)
    ppermute x3, waiting for transfers between devices, added_up(): acc = acc + lax.ppermute(acc, axis, swap)  223 us
    reduce_scatter x1, waiting for transfers between devices, shards(): lax.psum_scatter(jnp.dot(by_request, w_out, preferred_element_type=jnp.fl...  63.5 us
    pmax x1, blocking collectives, shards(): peak_score = lax.pmax(jnp.maximum(local_max, new_score), 'seq')  37.4 us
    unnamed x1, blocking collectives  33.8 us
    reduce_scatter x1, waiting for transfers between devices, shards(): lax.psum_scatter(scaled_out, 'seq', scatter_dimension=1, tiled=True)  29.6 us
    unnamed x49, local copies, waits for them, and re-layouts  22 us
    convert_element_type x1, other arithmetic, shards(): rotate_heads(summed + b_qkv[None, :], positions, col_start, HD, turned)  11.7 us
  transfers between devices with their start and end apart: 6, of which 5 were waited for; matrix products, arithmetic and copies ran while one was open for 5% of the time, Pallas kernels for 0%

profile of v1, /device:TPU:0, one launch (start us, length us, event | category | flops | bytes accessed | tf_op | source)
XLA Modules:
  0.0 519.9 jit_solution(12316151450606815911)
XLA Ops:
  6.5 9.0 %all_gather.6 = bf16[256,1024]{1,0:T(8,128)(2,1)S(1)} all-gather(bf16[64,1024]{1,0:T(8,128)(2,1)} %param.10), channel_id=1, replica_groups=mesh['seq'=8,'grp'=4] {'grp'}, dimensions={0}, use_global_device_ids=true | all-gather | bytes 655360 | tf_op jit(solution)/shard_map/all_gather | solution.py:62
  15.5 4.0 fusion.40
  19.5 1.6 collective-permute-start
  21.1 57.6 %collective-permute-done = f32[256,2560]{1,0:T(8,128)S(1)} collective-permute-done((f32[256,2560]{1,0:T(8,128)S(1)}, f32[256,2560]{1,0:T(8,128)S(1)}, u32[]{:S(2)}, u32[]{:S(2)}) %collective-permute-start) | collective-permute-done | bytes 2621472 | tf_op jit(solution)/shard_map/ppermute | solution.py:19
  79.1 1.6 collective-permute-start.1
  80.7 56.7 %collective-permute-done.1 = f32[256,2560]{1,0:T(8,128)S(1)} collective-permute-done((f32[256,2560]{1,0:T(8,128)S(1)}, f32[256,2560]{1,0:T(8,128)S(1)}, u32[]{:S(2)}, u32[]{:S(2)}) %collective-permute-start.1) | collective-permute-done | bytes 2621472 | tf_op jit(solution)/shard_map/ppermute | solution.py:19
  137.7 2.7 collective-permute-start.2
  140.8 0.8 gather_fusion
  141.6 0.6 gather_fusion.1
  142.9 0.6 select_reduce_fusion.2
  143.6 108.8 %collective-permute-done.2 = f32[256,2560]{1,0:T(8,128)} collective-permute-done((f32[256,2560]{1,0:T(8,128)S(1)}, f32[256,2560]{1,0:T(8,128)}, u32[]{:S(2)}, u32[]{:S(2)}) %collective-permute-start.2) | collective-permute-done | bytes 2621472 | tf_op jit(solution)/shard_map/ppermute | solution.py:19
  252.4 2.9 add_add_fusion
  255.3 2.3 copy.46
  257.6 2.0 slice_negate_fusion
  259.8 2.1 copy.47
  261.9 11.7 %select_convert_fusion = bf16[256,2560]{1,0:T(8,128)(2,1)S(1)} fusion(f32[256,2560]{1,0:T(8,128)} %copy-done.3, f32[256,2560]{1,0:T(8,128)} %copy.47, f32[2560]{0:T(1024)S(1)} %multiply_exponential_fusion, f32[256]{0:T(256)S(1)} %bitcast.120, f32[256]{0:T(256)S(1)} %bitcast.121, f32[256]{0:T(256)S(1)} %bitcast.119, ...), kind=kLoop, calls=%fused_computation.12 | loop fusion | flops 5242880 | bytes 6574592 | tf_op jit(solution)/shard_map/convert_element_type | solution.py:73
  273.6 2.5 gather_fusion.3
  276.1 3.5 all-to-all-start
  279.9 0.7 gather_fusion.2
  280.6 8.8 %copy.68 = bf16[512,8,8,128]{3,2,1,0:T(8,128)(2,1)} copy(bf16[512,8,8,128]{3,1,2,0:T(8,128)(2,1)} %bitcast.100) | data formatting | bytes 16777216
  289.4 8.8 %copy.69 = bf16[512,8,8,128]{3,2,1,0:T(8,128)(2,1)} copy(bf16[512,8,8,128]{3,1,2,0:T(8,128)(2,1)} %bitcast.101) | data formatting | bytes 16777216
  298.2 0.7 iota_compare_fusion.4
  299.0 1.0 copy.48
  300.5 1.7 gather_fusion.4
  302.2 1.2 copy.67
  303.4 6.9 %select_reduce_fusion.1 = (f32[32,8,8]{2,1,0:T(8,128)S(1)}, f32[32,8,8,128]{3,2,1,0:T(8,128)S(1)}) fusion(pred[32,128]{1,0:T(8,128)(4,1)S(1)} %fusion.25, bf16[32,8,8,128]{3,2,1,0:T(8,128)(2,1)S(1)} %bitcast.109, bf16[32,128,8,128]{3,2,1,0:T(8,128)(2,1)} %bitcast.97), kind=kOutput, calls=%fused_computation.26 | convolution fusion | flops 67893248 | bytes 9973760 | tf_op jit(solution)/shard_map/pkgd,ptkd->pkgt/dot_general | solution.py:103
  310.3 0.7 copy.51
  311.0 0.8 copy.53
  311.9 1.7 select_reduce_fusion
  313.5 2.0 gather_fusion.5
  315.6 1.5 copy.56
  317.0 0.7 slice_bitcast_fusion
  317.7 1.4 exponential_select_fusion
  319.4 1.0 reshape.359
  320.4 0.7 fusion.41
  321.3 37.4 %pmax.7 = f32[64,64]{0,1:T(8,128)S(1)} all-reduce(f32[64,64]{0,1:T(8,128)S(1)} %fusion.38), channel_id=1, replica_groups=mesh['seq'=8,'grp'=4] {'seq'}, use_global_device_ids=true, to_apply=%region_6.7 | all-reduce | flops 4096 | bytes 32768 | tf_op jit(solution)/shard_map/pmax | solution.py:150
  358.7 6.1 %fusion = f32[32,8,8,128]{3,2,1,0:T(8,128)S(1)} fusion(bf16[32,128,8,128]{3,2,1,0:T(8,128)(2,1)} %bitcast.96, f32[32,8,8,128]{3,2,1,0:T(8,128)S(1)} %get-tuple-element.21, f32[32,8,8]{2,1,0:T(8,128)S(1)} %get-tuple-element.20, pred[32,128]{1,0:T(8,128)(4,1)S(1)} %copy-done.8), kind=kOutput, calls=%fused_computation.7 | convolution fusion | flops 67895296 | bytes 10498048 | tf_op jit(solution)/shard_map/pkgt,ptkd->pkgd/dot_general | solution.py:112
  365.1 2.5 multiply_bitcast_fusion
  367.6 1.5 copy.96
  369.2 0.7 dynamic-slice
  370.6 0.7 fusion.11
  371.7 33.8 %all-reduce = f32[64,64]{0,1:T(8,128)S(1)} all-reduce(f32[64,64]{0,1:T(8,128)S(1)} %convolution_multiply_fusion), channel_id=3, replica_groups=mesh['seq'=8,'grp'=4] {'seq'}, use_global_device_ids=true, to_apply=%region_9.10.clone | all-reduce | flops 4096 | bytes 32768
  405.9 29.6 %reduce-scatter.3.cloned.1.call-done = f32[64,1024]{1,0:T(8,128)} async-done(((f32[64,8192]{1,0:T(8,128)}), f32[64,1024]{1,0:T(8,128)}) %reduce-scatter.3.cloned.1.call-update) | async-done | bytes 262160 | tf_op jit(solution)/shard_map/reduce_scatter | solution.py:156
  435.5 1.0 copy.73
  436.8 7.2 %all_gather.7 = bf16[256,1024]{1,0:T(8,128)(2,1)S(1)} all-gather(bf16[64,1024]{1,0:T(8,128)(2,1)S(1)} %bitcast.113), channel_id=1, replica_groups=mesh['seq'=8,'grp'=4] {'grp'}, dimensions={0}, use_global_device_ids=true | all-gather | bytes 655360 | tf_op jit(solution)/shard_map/all_gather | solution.py:170
  443.9 1.2 gather_fusion.6
  445.1 4.4 convolution_convert_fusion
  449.6 63.5 %reduce-scatter.5.cloned.1.call-done = bf16[32,2048]{1,0:T(8,128)(2,1)} async-done(((bf16[256,2048]{1,0:T(8,128)(2,1)}), bf16[32,2048]{1,0:T(8,128)(2,1)}) %reduce-scatter.5.cloned.1.call-update) | async-done | bytes 131088 | tf_op jit(solution)/shard_map/reduce_scatter | solution.py:172
  (82 shorter events, 4.8 us)
Async XLA Ops:
  6.5 135.0 %copy-start = (s32[256,128]{1,0:T(8,128)S(1)}, s32[256,128]{1,0:T(8,128)}, u32[]{:S(2)}) copy-start(s32[256,128]{1,0:T(8,128)} %param.17) | copy-start | bytes 393220
  19.5 59.2 %collective-permute-start = (f32[256,2560]{1,0:T(8,128)S(1)}, f32[256,2560]{1,0:T(8,128)S(1)}, u32[]{:S(2)}, u32[]{:S(2)}) collective-permute-start(f32[256,2560]{1,0:T(8,128)S(1)} %fusion.40), channel_id=1, source_target_pairs={{0,4},{4,0},{8,12},{12,8},{16,20},{20,16},{24,28},{28,24},{1,5},{5... | collective-permute-start | bytes 7864328 | tf_op jit(solution)/shard_map/ppermute | solution.py:19
  79.0 61.4 %copy-start.14 = (s32[256]{0:T(256)S(1)}, s32[256]{0:T(256)}, u32[]{:S(2)}) copy-start(s32[256]{0:T(256)} %param.19) | copy-start | bytes 3076
  79.0 61.7 %copy-start.2 = (s32[256]{0:T(256)S(1)}, s32[256]{0:T(256)}, u32[]{:S(2)}) copy-start(s32[256]{0:T(256)} %param.16) | copy-start | bytes 3076
  79.0 63.1 %copy-start.15 = (s32[3,256]{1,0:T(4,128)S(1)}, s32[3,256]{1,0:T(4,128)}, u32[]{:S(2)}) copy-start(s32[3,256]{1,0:T(4,128)} %param.18) | copy-start | bytes 9220
  79.0 173.3 %copy-start.10 = (f32[2560]{0:T(1024)S(1)}, f32[2560]{0:T(1024)}, u32[]{:S(2)}) copy-start(f32[2560]{0:T(1024)} %param.12) | copy-start | bytes 30724
  79.1 58.3 %collective-permute-start.1 = (f32[256,2560]{1,0:T(8,128)S(1)}, f32[256,2560]{1,0:T(8,128)S(1)}, u32[]{:S(2)}, u32[]{:S(2)}) collective-permute-start(f32[256,2560]{1,0:T(8,128)S(1)} %add.155), channel_id=1, source_target_pairs={{0,8},{4,12},{8,0},{12,4},{16,24},{20,28},{24,16},{28,20},{1,9},{5... | collective-permute-start | bytes 7864328 | tf_op jit(solution)/shard_map/ppermute | solution.py:19
  137.7 5.9 %copy-start.4 = (f32[256,2560]{1,0:T(8,128)}, f32[256,2560]{1,0:T(8,128)S(1)}, u32[]{:S(2)}) copy-start(f32[256,2560]{1,0:T(8,128)S(1)} %add.156) | copy-start | bytes 7864324
  137.7 114.7 %collective-permute-start.2 = (f32[256,2560]{1,0:T(8,128)S(1)}, f32[256,2560]{1,0:T(8,128)}, u32[]{:S(2)}, u32[]{:S(2)}) collective-permute-start(f32[256,2560]{1,0:T(8,128)S(1)} %add.156), channel_id=1, source_target_pairs={{0,16},{4,20},{8,24},{12,28},{16,0},{20,4},{24,8},{28,12},{1,17},{... | collective-permute-start | bytes 7864328 | tf_op jit(solution)/shard_map/ppermute | solution.py:19
  143.5 154.6 %copy-start.11 = (s32[32]{0:T(128)}, s32[32]{0:T(128)S(1)}, u32[]{:S(2)}) copy-start(s32[32]{0:T(128)S(1)} %get-tuple-element.6) | copy-start | bytes 388
  255.3 2.3 copy-start.3
  276.1 22.9 %all-to-all-start = ((bf16[4,64,2560]{2,1,0:T(8,128)(2,1)}), bf16[4,64,2560]{2,1,0:T(8,128)(2,1)S(1)}, u32[]{:S(2)}, u32[]{:S(2)}) async-start(bf16[4,64,2560]{2,1,0:T(8,128)(2,1)} %bitcast.8), calls=%async_computation | async-start | bytes 2621440 | tf_op jit(solution)/shard_map/all_to_all | solution.py:77
  279.6 155.9 %reduce-scatter.3.cloned.1.call-start = ((), (), s32[]{:S(2)}) async-start(), calls=%async_computation.3 | async-start | bytes 2359296 | tf_op jit(solution)/shard_map/reduce_scatter | solution.py:156
  279.9 20.6 %copy-start.13 = (s32[1024]{0:T(1024)}, s32[1024]{0:T(1024)S(1)}, u32[]{:S(2)}) copy-start(s32[1024]{0:T(1024)S(1)} %pad_clamp_fusion.2) | copy-start | bytes 12292
  298.2 2.0 copy-start.17
  298.9 4.4 copy-start.7
  317.7 3.5 copy-start.6
  319.1 39.5 %copy-start.8 = (pred[32,128]{1,0:T(8,128)(4,1)S(1)}, pred[32,128]{1,0:T(8,128)(4,1)}, u32[]{:S(2)}) copy-start(pred[32,128]{1,0:T(8,128)(4,1)} %copy-done.7) | copy-start | bytes 12292
  358.7 6.1 %copy-start.9 = (f32[32,64]{1,0:T(8,128)S(1)}, f32[32,64]{1,0:T(8,128)}, u32[]{:S(2)}) copy-start(f32[32,64]{1,0:T(8,128)} %exponential_select_fusion) | copy-start | bytes 24580
  358.7 6.4 %copy-start.12 = (s32[32]{0:T(128)S(1)}, s32[32]{0:T(128)}, u32[]{:S(2)}) copy-start(s32[32]{0:T(128)} %copy-done.11) | copy-start | bytes 388
  367.6 1.6 copy-start.18
  367.6 2.9 copy-start.16
  369.1 36.5 %copy-start.5 = (bf16[8,8,8,128]{3,1,2,0:T(8,128)(2,1)S(1)}, bf16[8,8,8,128]{3,1,2,0:T(8,128)(2,1)}, u32[]{:S(2)}) copy-start(bf16[8,8,8,128]{3,1,2,0:T(8,128)(2,1)} %get-tuple-element.13) | copy-start | bytes 393220
  369.1 143.9 %reduce-scatter.5.cloned.1.call-start = ((), (), s32[]{:S(2)}) async-start(), calls=%async_computation.4 | async-start | bytes 1179648 | tf_op jit(solution)/shard_map/reduce_scatter | solution.py:172
  443.9 69.1 %copy-start.1 = (s32[256,128]{1,0:T(8,128)S(1)}, s32[256,128]{1,0:T(8,128)}, u32[]{:S(2)}) copy-start(s32[256,128]{1,0:T(8,128)} %param.17) | copy-start | bytes 393220
Sparse Core Ops, SparseCore 0:
  369.2 66.2 reduce-scatter.2
  449.7 63.2 reduce-scatter.4
